TPU v7x, 32 devices: a whole 2x2x4 slice. The times are simulated.
32 devices in a mesh: tm: 8 (over y, x, core), panel: 4 (over z).
Axes of the slice: x: 2, y: 2, z: 4, core: 2. Of those that a mesh axis runs over, the one named last changes fastest.
Arguments:
- observed: bfloat16 [4096, 4096], P('tm', 'panel'), may hold values from -12 to 12
- present: int32 [32, 4096], P('tm', 'panel'), may hold values 0 or 1
- loadings: bfloat16 [4096, 256], P('panel'), may hold values from -0.09375 to 0.09375
- noise_var: float32 [4096], P('panel'), may hold values from 1 to 4
- decay_rate: float32 [256], replicated, may hold values from 2.4414063e-05 to 0.03
- panel_of_block: int32 [32], P('panel'), may hold values from 0 to 18
Outputs:
- smoothed: float32 [4096, 256], P('tm')
- loading_moment: float32 [256, 4096], P('tm', 'panel')
- state_moment: float32 [256, 256], replicated
- panel_var: float32 [19], replicated
All inputs are finite; a program needn't handle non-finite values. No bound on the sum of `present` on one device may be relied on, other than what follows from the above.
Results may differ from a plain program's by a relative error of at most 0.00055.
Values sent between devices are 32-bit elements; how exact they have to be, the bound alone decides.
A program may use at most 128 MiB of HBM per device.

v0:
```python
import math

import jax
import jax.numpy as jnp
from jax import lax
from jax.sharding import PartitionSpec as P

SER_BLOCK = 128
PANELS = 19
LEVELS = 7
BLOCK = 128


HIGH = lax.Precision.HIGHEST


def prefix_2(array, axis, combine, identity, reverse):
    peers, place = (lax.axis_size(axis), lax.axis_index(axis))
    everything = jax.tree.map(lambda part: lax.all_gather(part, axis), array)
    start = jax.tree.map(
        lambda part, zero: jnp.broadcast_to(jnp.asarray(zero, part.dtype), part.shape),
        array,
        identity,
    )

    def hop(k, before):
        at = peers - 1 - k if reverse else k
        reached = at > place if reverse else at < place
        new = combine(before, jax.tree.map(lambda part: part[at], everything))
        return jax.tree.map(lambda a, b: jnp.where(reached, a, b), new, before)

    return lax.fori_loop(0, peers, hop, start)


def invert_one(gram_block):
    identity = jnp.eye(gram_block.shape[0], dtype=jnp.float32)
    factor = jnp.linalg.cholesky(identity + gram_block)
    return jax.scipy.linalg.cho_solve((factor, True), identity)


def make_tables(gram_sum, persist):
    inverse = jax.vmap(invert_one)(gram_sum)
    transit = inverse * persist[None, None, :]
    powers = [transit]
    for level in range(LEVELS):
        powers.append(jnp.einsum("bij,bjk->bik", powers[-1], powers[-1], precision=HIGH))
    return (inverse, jnp.stack(powers, axis=1))


def doubling(values, powers, ahead):
    state_width = values.shape[1]
    for level in range(LEVELS):
        offset = 1 << level
        moved = jnp.dot(values, powers[level].T, precision=HIGH)
        zero_rows = jnp.zeros((offset, state_width), jnp.float32)
        if ahead:
            values = values + jnp.concatenate([zero_rows, moved[:-offset]], axis=0)
        else:
            values = values + jnp.concatenate([moved[offset:], zero_rows], axis=0)
    return values


def forward_pass(inputs, tables, carry_in):

    def forward_advance(state, block_pair):
        values, powers = block_pair
        values = values.at[0].add(jnp.dot(powers[0], state, precision=HIGH))
        values = doubling(values, powers, True)
        return (values[-1], values)

    last_state, outputs = lax.scan(forward_advance, carry_in, (inputs, tables))
    return (outputs, last_state)


def backward_pass(inputs, tables, carry_in):

    def backward_advance(state, block_pair):
        values, powers = block_pair
        values = values.at[-1].add(jnp.dot(powers[0], state, precision=HIGH))
        values = doubling(values, powers, False)
        return (values[0], values)

    first_state, outputs = lax.scan(backward_advance, carry_in, (inputs, tables), reverse=True)
    return (outputs, first_state)


def chain_combine(earlier, latter):
    return (
        jnp.dot(latter[0], earlier[0], precision=HIGH),
        jnp.dot(latter[0], earlier[1], precision=HIGH) + latter[1],
    )


def per_device(observed, present, loadings, noise_var, decay_rate, panel_of_block):
    time_rows, series = observed.shape
    state_width = loadings.shape[1]
    nblocks = time_rows // BLOCK
    loads = loadings.astype(jnp.float32)
    inv_noise = 1.0 / noise_var
    kept_mask = present.astype(jnp.float32)
    weighted = loads * inv_noise[:, None]
    gram_sum = jnp.einsum("bi,is,ir->bsr", kept_mask, weighted, loads, precision=HIGH)
    obs_kept = observed.astype(jnp.float32).reshape(nblocks, BLOCK, series) * kept_mask[:, None, :]
    projected = jnp.dot((obs_kept * inv_noise).reshape(time_rows, series), loads, precision=HIGH)
    persist = 1.0 - decay_rate
    gram_own = lax.psum_scatter(gram_sum, "panel", scatter_dimension=0, tiled=True)
    projected = lax.psum(projected, "panel")
    inverse_own, tables_own = make_tables(gram_own, persist)
    inverse, tables = (
        lax.all_gather(inverse_own, "panel", axis=0, tiled=True),
        lax.all_gather(tables_own, "panel", axis=0, tiled=True),
    )
    inputs = jnp.einsum(
        "bts,brs->btr", projected.reshape(nblocks, BLOCK, state_width), inverse, precision=HIGH
    )
    identity = jnp.eye(state_width, dtype=jnp.float32)
    zero_state = jnp.zeros((state_width,), jnp.float32)

    def compose(product_pair, powers):
        forward_map, backward_map = product_pair
        top_power = powers[LEVELS]
        following = (
            jnp.dot(top_power, forward_map, precision=HIGH),
            jnp.dot(backward_map, top_power, precision=HIGH),
        )
        return (following, None)

    (forward_map, backward_map), unused = lax.scan(compose, (identity, identity), tables)
    segments = lax.axis_size("tm")
    position = lax.axis_index("tm")
    is_last = position == segments - 1
    partial_filter, partial_end = forward_pass(inputs, tables, zero_state)
    prefix = prefix_2(
        (forward_map, partial_end), "tm", chain_combine, (identity, zero_state), False
    )
    filter_in = prefix[1]
    filtered, unused_end = forward_pass(inputs, tables, filter_in)
    offsets = filtered - jnp.einsum(
        "btr,bsr->bts", filtered * persist, tables[:, 0], precision=HIGH
    )
    offsets = offsets.at[-1, -1].set(jnp.where(is_last, filtered[-1, -1], offsets[-1, -1]))
    backward_map = backward_map * jnp.where(is_last, 0.0, 1.0)
    partial_smooth, partial_first = backward_pass(offsets, tables, zero_state)
    suffix = prefix_2(
        (backward_map, partial_first), "tm", chain_combine, (identity, zero_state), True
    )
    smooth_in = suffix[1]
    smooth_rows, unused_first = backward_pass(offsets, tables, smooth_in)
    smoothed = smooth_rows.reshape(time_rows, state_width)
    total_time = time_rows * segments
    flat_kept = obs_kept.reshape(time_rows, series)
    loading_moment = lax.psum_scatter(
        jnp.dot(smoothed.T, flat_kept, precision=HIGH) / math.sqrt(total_time),
        "tm",
        scatter_dimension=0,
        tiled=True,
    )
    local_moment = jnp.dot(smoothed.T, smoothed, precision=HIGH) / total_time
    state_moment = lax.psum(local_moment, "tm")
    fitted = (
        jnp.dot(smoothed, loads.T, precision=HIGH).reshape(nblocks, BLOCK, series)
        * kept_mask[:, None, :]
    )
    errors = obs_kept - fitted
    square_sums = jnp.sum(errors * errors, axis=(0, 1))
    obs_counts = BLOCK * jnp.sum(kept_mask, axis=0)
    onehot = (panel_of_block[:, None] == jnp.arange(PANELS, dtype=jnp.int32)[None, :]).astype(
        jnp.float32
    )
    panel_sums = jnp.dot(square_sums.reshape(-1, SER_BLOCK).sum(axis=1), onehot, precision=HIGH)
    panel_counts = jnp.dot(obs_counts.reshape(-1, SER_BLOCK).sum(axis=1), onehot, precision=HIGH)
    panel_sums, panel_counts = lax.psum((panel_sums, panel_counts), ("tm", "panel"))
    panel_var = panel_sums / jnp.maximum(panel_counts, 1.0)
    return (smoothed, loading_moment, state_moment, panel_var)


def solution(mesh):
    return jax.shard_map(
        per_device,
        mesh=mesh,
        in_specs=(
            P("tm", "panel"),
            P("tm", "panel"),
            P("panel", None),
            P("panel"),
            P(),
            P("panel"),
        ),
        out_specs=(P("tm", None), P("tm", "panel"), P(), P()),
        check_vma=False,
    )
```

profile of v0, /device:TPU:0, one launch (start us, length us, event | category | flops | bytes accessed | tf_op | source)
XLA Modules:
  0.0 615.7 jit_solution(15087279956974945775)
XLA Ops:
  11.4 4.7 fusion.113
  18.7 27.5 %reduce-scatter.3.cloned.1.call-done = f32[1,256,256]{1,2,0:T(8,128)} async-done(((f32[4,256,256]{1,2,0:T(8,128)}), f32[1,256,256]{1,2,0:T(8,128)}) %reduce-scatter.3.cloned.1.call-update) | async-done | bytes 262160 | tf_op jit(solution)/shard_map/reduce_scatter | solution.py:106
  48.3 11.7 %custom-call.20 = f32[1,128,128]{2,1,0:T(8,128)S(1)} custom-call(f32[1,128,128]{2,1,0:T(8,128)S(1)} %cholesky.117), custom_call_target="Cholesky" | custom-call | tf_op jit(solution)/shard_map/vmap(jit(cholesky))/cholesky | solution.py:37
  60.1 9.8 %custom-call.21 = f32[1,1,128,128]{2,3,1,0:T(8,128)S(1)} custom-call(f32[1,1,128,128]{3,2,1,0:T(8,128)S(1)} %get-tuple-element.871), custom_call_target="InvertDiagBlocksLowerTriangular" | custom-call | tf_op jit(solution)/shard_map/vmap(jit(cholesky))/cholesky | solution.py:37
  70.4 11.7 %custom-call.22 = f32[1,128,128]{2,1,0:T(8,128)S(1)} custom-call(f32[1,128,128]{2,1,0:T(8,128)S(1)} %fusion.123), custom_call_target="Cholesky" | custom-call | tf_op jit(solution)/shard_map/vmap(jit(cholesky))/cholesky | solution.py:37
  84.2 4.2 while.113
  88.4 19.7 %custom-call.23 = f32[1,2,128,128]{2,3,1,0:T(8,128)S(1)} custom-call(f32[1,2,128,128]{3,2,1,0:T(8,128)S(1)} %bitcast.497), custom_call_target="InvertDiagBlocksLowerTriangular" | custom-call | tf_op jit(solution)/shard_map/vmap(jit(_cho_solve))/triangular_solve | solution.py:38
  115.1 22.3 %all-gather.13.cloned.1.call-done = f32[4,256,256]{2,1,0:T(8,128)} async-done(((f32[1,256,256]{2,1,0:T(8,128)}), f32[4,256,256]{2,1,0:T(8,128)}) %all-gather.13.cloned.1.call-update) | async-done | bytes 1048592 | tf_op jit(solution)/shard_map/all_gather | solution.py:110
  137.4 2.5 fusion.152
  139.9 147.9 %all-gather.11.cloned.1.call-done = f32[4,8,256,256]{3,2,1,0:T(8,128)} async-done(((f32[1,8,256,256]{3,2,1,0:T(8,128)}), f32[4,8,256,256]{3,2,1,0:T(8,128)}) %all-gather.11.cloned.1.call-update) | async-done | bytes 8388624 | tf_op jit(solution)/shard_map/all_gather | solution.py:111
  287.8 11.9 %while.108 = (s32[]{:T(128)}, f32[256,256]{1,0:T(8,128)S(1)}, f32[256,256]{0,1:T(8,128)S(1)}, f32[4,8,256,256]{3,2,1,0:T(8,128)}, s32[]{:T(128)}, /*index=5*/s32[]{:T(128)}, s32[]{}) while((s32[]{:T(128)}, f32[256,256]{1,0:T(8,128)S(1)}, f32[256,256]{0,1:T(8,128)S(1)}, f32[4,8,256,256]{3,2,1,0:T(8,128)}, s32[]{:T(128)}, /*index=5*/s32[]{:T(128)}, ...), condition=%wide.region_6.7_spmd, body=%wide.region_5.6_spmd.sunk | while | flops 402653184 | bytes 2622561 | solution.py:128
  300.5 44.1 %while.109 = (s32[]{:T(128)}, f32[256]{0:T(256)S(1)}, f32[4,128,256]{2,1,0:T(8,128)S(1)}, f32[4,8,256,256]{3,2,1,0:T(8,128)}, s32[]{:T(128)}, /*index=5*/s32[]{:...) while((s32[]{:T(128)}, f32[256]{0:T(256)S(1)}, f32[4,128,256]{2,1,0:T(8,128)S(1)}, ...), condition=%wide.region_9.10_spmd, body=%wide.region_8.9_spmd.sunk | while | flops 605749760 | bytes 6317305 | solution.py:71
  344.5 9.0 %all-gather.4 = f32[8,1,256]{2,1,0:T(1,128)S(1)} all-gather(f32[1,1,256]{2,1,0:T(1,128)S(1)} %bitcast.491), channel_id=4, replica_groups=mesh['tm'=8,'panel'=4] {'tm'}, dimensions={0}, use_global_device_ids=true | all-gather | bytes 9216 | tf_op jit(solution)/shard_map/all_gather | solution.py:19
  354.3 11.0 %while.114 = (s32[]{:T(128)}, f32[256]{0:T(256)S(1)}, s32[]{:T(128)}, f32[8,256,256]{2,1,0:T(8,128)}, f32[8,256]{1,0:T(8,128)S(1)}, /*index=5*/s32[]{:T(128)}, s32[]{:T(128)}) while((s32[]{:T(128)}, f32[256]{0:T(256)S(1)}, s32[]{:T(128)}, f32[8,256,256]{2,1,0:T(8,128)}, f32[8,256]{1,0:T(8,128)S(1)}, /*index=5*/s32[]{:T(128)}, ...), condition=%wide.region_11.12_spmd.clone, body=%wide.region_10.11_spmd.clone.sunk | while | flops 787460 | bytes 272998 | solution.py:32
  365.4 44.2 %while.110 = (s32[]{:T(128)}, f32[256]{0:T(256)S(1)}, f32[4,128,256]{2,1,0:T(8,128)S(1)}, f32[4,128,256]{2,1,0:T(8,128)S(1)}, f32[4,8,256,256]{3,2,1,0:T(8,128)}...) while((s32[]{:T(128)}, f32[256]{0:T(256)S(1)}, ...), condition=%wide.region_13.14_spmd, body=%wide.region_12.13_spmd.sunk | while | flops 605782272 | bytes 6710533 | solution.py:71
  409.6 2.4 convolution_subtract_fusion
  412.0 44.1 %while.111 = (s32[]{:T(128)}, f32[256]{0:T(256)S(1)}, f32[4,128,256]{2,1,0:T(8,128)S(1)}, f32[4,8,256,256]{3,2,1,0:T(8,128)}, s32[]{:T(128)}, /*index=5*/s32[]{:...) while((s32[]{:T(128)}, f32[256]{0:T(256)S(1)}, ...), condition=%wide.region_15.16_spmd, body=%wide.region_14.15_spmd.sunk | while | flops 605749760 | bytes 6313261 | solution.py:83
  456.1 8.9 %all-gather.5 = f32[8,1,256]{2,1,0:T(1,128)S(1)} all-gather(f32[1,1,256]{2,1,0:T(1,128)S(1)} %bitcast.494), channel_id=5, replica_groups=mesh['tm'=8,'panel'=4] {'tm'}, dimensions={0}, use_global_device_ids=true | all-gather | bytes 9216 | tf_op jit(solution)/shard_map/all_gather | solution.py:19
  466.9 3.2 while.115
  470.2 44.3 %while.112 = (s32[]{:T(128)}, f32[256]{0:T(256)S(1)}, f32[4,128,256]{2,1,0:T(8,128)S(1)}, f32[4,128,256]{2,1,0:T(8,128)S(1)}, f32[4,8,256,256]{3,2,1,0:T(8,128)}...) while((s32[]{:T(128)}, f32[256]{0:T(256)S(1)}, ...), condition=%wide.region_19.20_spmd, body=%wide.region_18.19_spmd.sunk | while | flops 605782272 | bytes 6706489 | solution.py:83
  516.6 2.9 fusion.116
  521.5 37.4 %all-reduce.29 = (f32[19]{0:T(128)S(1)}, f32[19]{0:T(128)S(1)}) all-reduce(f32[19]{0:T(128)S(1)} %convolution_bitcast_fusion.6, f32[19]{0:T(128)S(1)} %convolution_bitcast_fusion.5), channel_id=1, replica_groups=mesh['tm'=8,'panel'=4] {'tm','panel'}, use_global_device_ids=true, to_apply=%region_24.25 | all-reduce | flops 38 | bytes 304 | tf_op jit(solution)/shard_map/psum | solution.py:172
  559.5 8.1 %all-reduce.35.cloned.1.call-done = f32[256,256]{1,0:T(8,128)} async-done(((f32[256,256]{1,0:T(8,128)}), f32[256,256]{1,0:T(8,128)}) %all-reduce.35.cloned.1.call-update) | async-done | bytes 262160 | tf_op jit(solution)/shard_map/psum | solution.py:159
  567.6 39.1 %reduce-scatter.5.cloned.1.call-done = f32[32,1024]{1,0:T(8,128)} async-done(((f32[256,1024]{1,0:T(8,128)}), f32[32,1024]{1,0:T(8,128)}) %reduce-scatter.5.cloned.1.call-update) | async-done | bytes 131088 | tf_op jit(solution)/shard_map/reduce_scatter | solution.py:152
  (496 shorter events, 230.0 us)
Async XLA Ops:
  7.2 9.3 %copy-start.5 = (bf16[1024,256]{1,0:T(8,128)(2,1)S(1)}, bf16[1024,256]{1,0:T(8,128)(2,1)}, u32[]{:S(2)}) copy-start(bf16[1024,256]{1,0:T(8,128)(2,1)} %param.32) | copy-start | bytes 1572868
  7.2 8.9 %copy-start.2 = (bf16[512,1024]{1,0:T(8,128)(2,1)S(1)}, bf16[512,1024]{1,0:T(8,128)(2,1)}, u32[]{:S(2)}) copy-start(bf16[512,1024]{1,0:T(8,128)(2,1)} %param.30) | copy-start | bytes 3145732
  7.2 11.5 %copy-start.7 = (f32[256]{0:T(256)S(1)}, f32[256]{0:T(256)}, u32[]{:S(2)}) copy-start(f32[256]{0:T(256)} %param.34) | copy-start | bytes 3076
  7.2 39.0 %reduce-scatter.3.cloned.1.call-start = ((), (), s32[]{:S(2)}) async-start(), calls=%async_computation.2 | async-start | bytes 1310720 | tf_op jit(solution)/shard_map/reduce_scatter | solution.py:106
  16.1 99.0 %all-reduce.33.cloned.1.call-start = ((), (), s32[]{:S(2)}) async-start(), calls=%async_computation.4 | async-start | bytes 1048576 | tf_op jit(solution)/shard_map/psum | solution.py:107
  18.4 119.0 %all-gather.13.cloned.1.call-start = ((), (), s32[]{:S(2)}) async-start(), calls=%async_computation.5 | async-start | bytes 1310720 | tf_op jit(solution)/shard_map/all_gather | solution.py:110
  110.7 177.1 %all-gather.11.cloned.1.call-start = ((), (), s32[]{:S(2)}) async-start(), calls=%async_computation.3 | async-start | bytes 10485760 | tf_op jit(solution)/shard_map/all_gather | solution.py:111
  113.5 1.3 copy-start.4
  114.8 239.5 %all-gather.17.cloned.1.call-start = ((), (), s32[]{:S(2)}) async-start(), calls=%async_computation.9 | async-start | bytes 2359296 | tf_op jit(solution)/shard_map/all_gather | solution.py:19
  299.7 0.7 copy-start
  300.4 164.6 %all-gather.15.cloned.1.call-start = ((), (), s32[]{:S(2)}) async-start(), calls=%async_computation.8 | async-start | bytes 2359296 | tf_op jit(solution)/shard_map/all_gather | solution.py:19
  354.3 213.3 %all-reduce.35.cloned.1.call-start = ((), (), s32[]{:S(2)}) async-start(), calls=%async_computation.7 | async-start | bytes 524288 | tf_op jit(solution)/shard_map/psum | solution.py:159
  470.2 46.4 %copy-start.3 = (bf16[512,1024]{1,0:T(8,128)(2,1)S(1)}, bf16[512,1024]{1,0:T(8,128)(2,1)}, u32[]{:S(2)}) copy-start(bf16[512,1024]{1,0:T(8,128)(2,1)} %param.30) | copy-start | bytes 3145732
  470.2 49.4 %copy-start.6 = (s32[4,1024]{1,0:T(4,128)S(1)}, s32[4,1024]{1,0:T(4,128)}, u32[]{:S(2)}) copy-start(s32[4,1024]{1,0:T(4,128)} %param.31) | copy-start | bytes 49156
  470.2 49.5 %copy-start.8 = (s32[8]{0:T(128)S(1)}, s32[8]{0:T(128)}, u32[]{:S(2)}) copy-start(s32[8]{0:T(128)} %param.35) | copy-start | bytes 100
  514.5 93.9 %copy-start.1 = (f32[4,128,256]{2,1,0:T(8,128)}, f32[4,128,256]{2,1,0:T(8,128)S(1)}, u32[]{:S(2)}) copy-start(f32[4,128,256]{2,1,0:T(8,128)S(1)} %get-tuple-element.731) | copy-start | bytes 1572868
  516.3 90.4 %reduce-scatter.5.cloned.1.call-start = ((), (), s32[]{:S(2)}) async-start(), calls=%async_computation.6 | async-start | bytes 1179648 | tf_op jit(solution)/shard_map/reduce_scatter | solution.py:152
Sparse Core Ops, SparseCore 0:
  16.2 29.9 reduce-scatter.2
  49.1 37.3 all-reduce.32
  110.8 26.4 all-gather.12
  138.8 148.9 all-gather.10
  300.5 25.9 all-gather.16
  354.4 25.3 all-gather.14
  516.4 51.1 all-reduce.34
  571.3 35.3 reduce-scatter.4
where the time goes:
time: 624 us; the launch traced here: 616 us
  waiting for transfers between devices  245 us (39%)
  matrix products  217 us (35%)
  other arithmetic  63.8 us (10%)
  blocking collectives  55.3 us (9%)
  between operations  16.5 us (3%)
  local copies, waits for them, and re-layouts  13.9 us (2%)
    dot_general x112, matrix products, doubling(): moved = jnp.dot(values, powers[level].T, precision=HIGH)  151 us
    all_gather x1, waiting for transfers between devices, per_device(): lax.all_gather(tables_own, 'panel', axis=0, tiled=True)  148 us
    reduce_scatter x1, waiting for transfers between devices, per_device(): lax.psum_scatter(jnp.dot(smoothed.T, flat_kept, precision=HIGH) / math.sq...  39.1 us
    psum x1, blocking collectives, per_device(): lax.psum((panel_sums, panel_counts), ('tm', 'panel'))  37.4 us
    another operation x6, other arithmetic, invert_one(): factor = jnp.linalg.cholesky(identity + gram_block)  34 us
    reduce_scatter x1, waiting for transfers between devices, per_device(): lax.psum_scatter(gram_sum, 'panel', scatter_dimension=0, tiled=True)  27.5 us
    all_gather x1, waiting for transfers between devices, per_device(): lax.all_gather(inverse_own, 'panel', axis=0, tiled=True)  22.3 us
    another operation x4, other arithmetic, invert_one(): return jax.scipy.linalg.cho_solve((factor, True), identity)  20.4 us
  transfers between devices with their start and end apart: 8, of which 5 were waited for; matrix products, arithmetic and copies ran while one was open for 36% of the time, Pallas kernels for 0%

commit v1 on v0

v1 whole, which is shorter than its diff:
```python
import functools
import math

import jax
import jax.numpy as jnp
from jax import lax
from jax.experimental import pallas as pl
from jax.experimental.pallas import tpu as pltpu
from jax.sharding import PartitionSpec as P

SER_BLOCK = 128
PANELS = 19
LEVELS = 7
BLOCK = 128
PAD = 8

HIGH = lax.Precision.HIGHEST
MESH = pl.DeviceIdType.MESH
VMEM_LIMIT = 60 * 1024 * 1024


def mm(a, b):
    return jnp.dot(a, b, precision=HIGH, preferred_element_type=jnp.float32)


def mm_t(a, b):
    return lax.dot_general(
        a, b, (((1,), (1,)), ((), ())), precision=HIGH, preferred_element_type=jnp.float32
    )


def vmem(n):
    return [pl.BlockSpec(memory_space=pltpu.VMEM)] * n


def params(collective_id=None):
    if collective_id is None:
        return pltpu.CompilerParams(vmem_limit_bytes=VMEM_LIMIT)
    return pltpu.CompilerParams(
        vmem_limit_bytes=VMEM_LIMIT, collective_id=collective_id, has_side_effects=True
    )


def send_all(axis, n, me, source, target, send, recv):
    def one(d, unused):
        peer = lax.rem(me + d, n)
        pltpu.make_async_remote_copy(
            src_ref=source(peer),
            dst_ref=target(me, d),
            send_sem=send.at[d - 1],
            recv_sem=recv.at[d - 1],
            device_id={axis: peer},
            device_id_type=MESH,
        ).start()
        return unused

    lax.fori_loop(1, n, one, 0)


def wait_all(axis, n, me, source, target, send, recv):
    def one(d, unused):
        origin = lax.rem(me + n - d, n)
        copy = pltpu.make_async_remote_copy(
            src_ref=source(lax.rem(me + d, n)),
            dst_ref=target(origin, d),
            send_sem=send.at[d - 1],
            recv_sem=recv.at[d - 1],
            device_id={axis: origin},
            device_id_type=MESH,
        )
        copy.wait_recv()
        copy.wait_send()
        return unused

    lax.fori_loop(1, n, one, 0)


def greet(groups):
    barrier = pltpu.get_barrier_semaphore()
    total = 0
    for axis, n, me in groups:

        def one(d, unused, axis=axis, n=n, me=me):
            pl.semaphore_signal(
                barrier, inc=1, device_id={axis: lax.rem(me + d, n)}, device_id_type=MESH
            )
            return unused

        lax.fori_loop(1, n, one, 0)
        total += n - 1
    pl.semaphore_wait(barrier, total)


def scatter_kernel(panels, parts, out, landed, send, recv):
    me = lax.axis_index("panel")
    greet([("panel", panels, me)])
    args = ("panel", panels, me, lambda peer: parts.at[peer], lambda i, d: landed.at[d - 1])
    send_all(*args, send, recv)
    total = parts[me]
    wait_all(*args, send, recv)
    for d in range(panels - 1):
        total = total + landed[d]
    out[...] = total


def scatter_panel(parts):
    panels = parts.shape[0]
    shape = parts.shape[1:]
    return pl.pallas_call(
        functools.partial(scatter_kernel, panels),
        out_shape=jax.ShapeDtypeStruct(shape, jnp.float32),
        in_specs=vmem(1),
        out_specs=pl.BlockSpec(memory_space=pltpu.VMEM),
        scratch_shapes=[
            pltpu.VMEM((panels - 1,) + shape, jnp.float32),
            pltpu.SemaphoreType.DMA((panels - 1,)),
            pltpu.SemaphoreType.DMA((panels - 1,)),
        ],
        compiler_params=params(1),
        name="scatter_panel",
    )(parts)


def shift_rows(moved, offset, ahead):
    rows = moved.shape[0]
    zero = jnp.zeros((offset, moved.shape[1]), jnp.float32)
    if offset % 8 == 0:
        if ahead:
            return jnp.concatenate([zero, moved[: rows - offset]], axis=0)
        return jnp.concatenate([moved[offset:], zero], axis=0)
    row = lax.broadcasted_iota(jnp.int32, moved.shape, 0)
    if ahead:
        return jnp.where(row >= offset, pltpu.roll(moved, offset, 0), 0.0)
    return jnp.where(row < rows - offset, pltpu.roll(moved, rows - offset, 0), 0.0)


def local_kernel(reduced, rho, pack, powers, values_out, stack):
    width = reduced.shape[1]
    gram = reduced[:width]
    eye = (
        lax.broadcasted_iota(jnp.int32, (width, width), 0)
        == lax.broadcasted_iota(jnp.int32, (width, width), 1)
    ).astype(jnp.float32)
    bound = jnp.max(jnp.sum(jnp.abs(gram), axis=1))
    alpha = 2.0 / (2.0 + bound)
    rest = eye - alpha * (eye + gram)
    stack[:width] = eye + rest
    stack[width:] = mm(rest, rest)
    ratio = bound / (2.0 + bound)

    def step(level):
        grown = mm(stack[...], stack[width:])
        stack[:width] = stack[:width] + grown[:width]
        stack[width:] = grown[width:]
        return level * level

    lax.while_loop(lambda level: level > 1e-5, step, ratio * ratio)
    guess = alpha * stack[:width]
    inverse = guess + mm(guess, (eye - guess) - mm(gram, guess))
    values = mm(reduced[width:], inverse)
    power = rho[...] * inverse
    for level in range(LEVELS):
        powers[level] = power
        both = mm(jnp.concatenate([power, values], axis=0), power)
        values = values + shift_rows(both[width:], 1 << level, True)
        power = both[:width]
    values_out[...] = values
    pack[:width] = power
    row = lax.broadcasted_iota(jnp.int32, (PAD, width), 0)
    pack[width:] = jnp.where(row == 0, pltpu.roll(values[BLOCK - PAD :], 1, 0), 0.0)


def local_tables(reduced, persist):
    width = reduced.shape[1]
    f32 = jnp.float32
    return pl.pallas_call(
        local_kernel,
        out_shape=(
            jax.ShapeDtypeStruct((width + PAD, width), f32),
            jax.ShapeDtypeStruct((LEVELS, width, width), f32),
            jax.ShapeDtypeStruct((BLOCK, width), f32),
        ),
        in_specs=vmem(2),
        out_specs=tuple(vmem(3)),
        scratch_shapes=[pltpu.VMEM((2 * width, width), f32)],
        compiler_params=params(),
        name="local_tables",
    )(reduced, persist[:, None])


def spread(first, powers, ahead):
    rows = mm(first, powers[0])
    if not ahead:
        rows = pltpu.roll(rows, PAD - 1, 0)
    for level in range(LEVELS):
        moved = mm(rows, powers[level])
        if level < 3:
            offset = 1 << level
            rows = rows + pltpu.roll(moved, offset if ahead else PAD - offset, 0)
        elif ahead:
            rows = jnp.concatenate([rows, moved], axis=0)
        else:
            rows = jnp.concatenate([moved, rows], axis=0)
    return rows


def smooth_kernel(
    segments,
    panels,
    pack,
    powers,
    partial,
    rho,
    out,
    near,
    far,
    seg_pack,
    own_first,
    firsts,
    seg_first,
    seg_firsts,
    mine,
    near_send,
    near_recv,
    far_send,
    far_recv,
):
    width = pack.shape[1]
    place = lax.axis_index("panel")
    segment = lax.axis_index("tm")
    greet([("panel", panels, place), ("tm", segments, segment)])

    def gather(axis, n, me, source, target, stage):
        send, recv = (near_send, near_recv) if axis == "panel" else (far_send, far_recv)
        args = (axis, n, me, lambda peer: source, lambda i, d: target.at[i])
        send_all(*args, send.at[stage], recv.at[stage])
        target[me] = source[...]
        wait_all(*args, send.at[stage], recv.at[stage])

    row = lax.broadcasted_iota(jnp.int32, (PAD, width), 0)
    decay = rho[...]
    gather("panel", panels, place, pack, near, 0)
    whole = near[0]
    keep = (lax.broadcasted_iota(jnp.int32, (width + PAD, width), 0) >= width).astype(jnp.float32)
    for k in range(1, panels):
        whole = mm(whole, near[k, :width]) + keep * near[k]
    seg_pack[...] = whole
    gather("tm", segments, segment, seg_pack, far, 0)

    def far_ahead(k, state):
        new = mm(state, far[k, :width]) + far[k, width:]
        return jnp.where(k < segment, new, state)

    state = lax.fori_loop(0, segments - 1, far_ahead, jnp.zeros((PAD, width), jnp.float32))
    for k in range(panels - 1):
        state = jnp.where(k < place, mm(state, near[k, :width]) + near[k, width:], state)

    filtered = partial[...] + spread(state, powers, True)
    values = filtered - mm(filtered * decay, powers[0])
    last = jnp.logical_and(segment == segments - 1, place == panels - 1)
    final_row = lax.broadcasted_iota(jnp.int32, (BLOCK, width), 0) == BLOCK - 1
    values = jnp.where(jnp.logical_and(final_row, last), filtered, values)
    for level in range(LEVELS):
        values = values + shift_rows(mm(values, powers[level]), 1 << level, False)
    own_first[...] = jnp.where(row == 0, values[:PAD], 0.0)
    gather("panel", panels, place, own_first, firsts, 1)
    total = firsts[panels - 1]
    for k in range(panels - 2, -1, -1):
        total = mm(total, near[k, :width]) + firsts[k]
    seg_first[...] = total * decay
    gather("tm", segments, segment, seg_first, seg_firsts, 1)

    def far_back(j, state):
        k = segments - 1 - j
        new = mm_t(state, far[k, :width]) + seg_firsts[k]
        return jnp.where(k > segment, new, state)

    state = lax.fori_loop(0, segments - 1, far_back, jnp.zeros((PAD, width), jnp.float32))
    state = state / decay
    for k in range(panels - 1, 0, -1):
        state = jnp.where(k > place, mm(state, near[k, :width]) + firsts[k], state)
    mine[...] = values + spread(state, powers, False)
    gather("panel", panels, place, mine, out, 2)


def smooth(pack, powers, partial, persist):
    width = pack.shape[1]
    segments, panels = lax.axis_size("tm"), lax.axis_size("panel")
    f32 = jnp.float32
    return pl.pallas_call(
        functools.partial(smooth_kernel, segments, panels),
        out_shape=jax.ShapeDtypeStruct((panels, BLOCK, width), f32),
        in_specs=vmem(4),
        out_specs=pl.BlockSpec(memory_space=pltpu.VMEM),
        scratch_shapes=[
            pltpu.VMEM((panels, width + PAD, width), f32),
            pltpu.VMEM((segments, width + PAD, width), f32),
            pltpu.VMEM((width + PAD, width), f32),
            pltpu.VMEM((PAD, width), f32),
            pltpu.VMEM((panels, PAD, width), f32),
            pltpu.VMEM((PAD, width), f32),
            pltpu.VMEM((segments, PAD, width), f32),
            pltpu.VMEM((BLOCK, width), f32),
            pltpu.SemaphoreType.DMA((3, panels - 1)),
            pltpu.SemaphoreType.DMA((3, panels - 1)),
            pltpu.SemaphoreType.DMA((2, segments - 1)),
            pltpu.SemaphoreType.DMA((2, segments - 1)),
        ],
        compiler_params=params(2),
        name="smooth",
    )(pack, powers, partial, persist[None, :])


def finish_kernel(
    segments, panels, cross, moment, sums, out, gathered, landed, moments, bundle, *sems
):
    c_send, c_recv, m_send, m_recv, g_send, g_recv = sems
    place = lax.axis_index("panel")
    segment = lax.axis_index("tm")
    devices = segments * panels
    me = place * segments + segment
    rows = moment.shape[1]
    barrier = pltpu.get_barrier_semaphore()

    def where(d):
        peer = lax.rem(me + d, devices)
        return {"tm": lax.rem(peer, segments), "panel": peer // segments}

    def hello(d, unused):
        pl.semaphore_signal(barrier, inc=1, device_id=where(d), device_id_type=MESH)
        return unused

    lax.fori_loop(1, devices, hello, 0)
    pl.semaphore_wait(barrier, devices - 1)

    m_args = ("tm", segments, segment, lambda i: moment.at[i], lambda i, d: moments.at[d - 1])
    c_args = ("tm", segments, segment, lambda i: cross.at[i], lambda i, d: landed.at[d - 1])
    send_all(*m_args, m_send, m_recv)
    send_all(*c_args, c_send, c_recv)
    own = moment[segment]
    wait_all(*m_args, m_send, m_recv)
    for d in range(segments - 1):
        own = own + moments[d]
    bundle[:rows] = own
    bundle[rows:] = sums[...]
    gathered[me] = bundle[...]

    def copy(d, slot):
        return pltpu.make_async_remote_copy(
            src_ref=bundle,
            dst_ref=gathered.at[slot],
            send_sem=g_send.at[d - 1],
            recv_sem=g_recv.at[d - 1],
            device_id=where(d),
            device_id_type=MESH,
        )

    def push(d, unused):
        copy(d, me).start()
        return unused

    lax.fori_loop(1, devices, push, 0)
    total = cross[segment]
    wait_all(*c_args, c_send, c_recv)
    for d in range(segments - 1):
        total = total + landed[d]
    out[...] = total

    def pull(d, unused):
        got = copy(d, lax.rem(me + devices - d, devices))
        got.wait_recv()
        got.wait_send()
        return unused

    lax.fori_loop(1, devices, pull, 0)


def finish(cross, moment, sums):
    segments, panels = lax.axis_size("tm"), lax.axis_size("panel")
    devices = segments * panels
    f32 = jnp.float32
    rows = moment.shape[1] + sums.shape[0]
    dma = pltpu.SemaphoreType.DMA
    return pl.pallas_call(
        functools.partial(finish_kernel, segments, panels),
        out_shape=(
            jax.ShapeDtypeStruct(cross.shape[1:], f32),
            jax.ShapeDtypeStruct((devices, rows, 128), f32),
        ),
        in_specs=vmem(3),
        out_specs=tuple(vmem(2)),
        scratch_shapes=[
            pltpu.VMEM((segments - 1,) + cross.shape[1:], f32),
            pltpu.VMEM((segments - 1,) + moment.shape[1:], f32),
            pltpu.VMEM((rows, 128), f32),
            dma((segments - 1,)),
            dma((segments - 1,)),
            dma((segments - 1,)),
            dma((segments - 1,)),
            dma((devices - 1,)),
            dma((devices - 1,)),
        ],
        compiler_params=params(3),
        name="finish",
    )(cross, moment, sums)


def per_device(observed, present, loadings, noise_var, decay_rate, panel_of_block):
    time_rows, series = observed.shape
    width = loadings.shape[1]
    nblocks = time_rows // BLOCK
    segments, panels = lax.axis_size("tm"), lax.axis_size("panel")
    assert nblocks == panels
    loads = loadings.astype(jnp.float32)
    inv_noise = 1.0 / noise_var
    kept_mask = present.astype(jnp.float32)
    weighted = loads * inv_noise[:, None]
    gram_sum = jnp.einsum("bi,is,ir->bsr", kept_mask, weighted, loads, precision=HIGH)
    obs_kept = observed.astype(jnp.float32).reshape(nblocks, BLOCK, series) * kept_mask[:, None, :]
    projected = jnp.dot((obs_kept * inv_noise).reshape(time_rows, series), loads, precision=HIGH)
    persist = 1.0 - decay_rate
    parts = jnp.concatenate([gram_sum, projected.reshape(nblocks, BLOCK, width)], axis=1)
    reduced = scatter_panel(parts)
    pack, powers, partial = local_tables(reduced, persist)
    smoothed = smooth(pack, powers, partial, persist).reshape(time_rows, width)

    total_time = time_rows * segments
    flat_kept = obs_kept.reshape(time_rows, series)
    cross = jnp.dot(smoothed.T, flat_kept, precision=HIGH) / math.sqrt(total_time)
    part = width // panels
    columns = lax.dynamic_slice_in_dim(smoothed, lax.axis_index("panel") * part, part, axis=1)
    moment = jnp.dot(columns.T, smoothed, precision=HIGH) / total_time
    fitted = (
        jnp.dot(smoothed, loads.T, precision=HIGH).reshape(nblocks, BLOCK, series)
        * kept_mask[:, None, :]
    )
    errors = obs_kept - fitted
    square_sums = jnp.sum(errors * errors, axis=(0, 1))
    obs_counts = BLOCK * jnp.sum(kept_mask, axis=0)
    onehot = panel_of_block[:, None] == jnp.arange(128, dtype=jnp.int32)[None, :]
    block_sums = square_sums.reshape(-1, SER_BLOCK).sum(axis=1)
    block_counts = obs_counts.reshape(-1, SER_BLOCK).sum(axis=1)
    sums = jnp.stack(
        [
            jnp.sum(jnp.where(onehot, block_sums[:, None], 0.0), axis=0),
            jnp.sum(jnp.where(onehot, block_counts[:, None], 0.0), axis=0),
        ]
    )
    sums = jnp.concatenate([sums, jnp.zeros((PAD - 2, 128), jnp.float32)], axis=0)
    moment_rows = part * width // segments // 128
    loading_moment, gathered = finish(
        cross.reshape(segments, width // segments, series),
        moment.reshape(segments, moment_rows, 128),
        sums,
    )
    state_moment = gathered[:, :moment_rows].reshape(width, width)
    totals = jnp.sum(gathered[:, moment_rows : moment_rows + 2, :PANELS], axis=0)
    panel_var = totals[0] / jnp.maximum(totals[1], 1.0)
    return (smoothed, loading_moment, state_moment, panel_var)


def solution(mesh):
    return jax.shard_map(
        per_device,
        mesh=mesh,
        in_specs=(
            P("tm", "panel"),
            P("tm", "panel"),
            P("panel", None),
            P("panel"),
            P(),
            P("panel"),
        ),
        out_specs=(P("tm", None), P("tm", "panel"), P(), P()),
        check_vma=False,
    )
```

time: 624 us -> 187 us (0.30); the launches traced: 616 us -> 187 us
  waiting for transfers between devices: 245 us -> 0 us
  matrix products: 217 us -> 9.27 us
  Pallas kernels: 0 us -> 165 us
  other arithmetic: 63.8 us -> 6.84 us
  blocking collectives: 55.3 us -> 0 us
  between operations: 16.5 us -> 0.85 us
  local copies, waits for them, and re-layouts: 13.9 us -> 5.12 us
    dot_general x164 -> x1, matrix products: 204 us -> 0.68 us  [per_device(): moment = jnp.dot(columns.T, smoothed, precision=HIGH) / total_time]
    all_gather x4 -> x0, waiting for transfers between devices: 170 us -> none  [the longest x1 148 us: per_device(): lax.all_gather(tables_own, 'panel', axis=0, tiled=True)]
    pallas_call x0 -> x4, Pallas kernels: none -> 165 us  [the longest x1 93 us: smooth(): pl.pallas_call(functools.partial(smooth_kernel, segments, panels), out_sh...]
    reduce_scatter x2 -> x0, waiting for transfers between devices: 66.7 us -> none  [the longest x1 39.1 us: per_device(): lax.psum_scatter(jnp.dot(smoothed.T, flat_kept, precision=HIGH) / math.sq...]
    another operation x10 -> x0, other arithmetic: 54.4 us -> none  [the longest x6 34 us: invert_one(): factor = jnp.linalg.cholesky(identity + gram_block)]
    psum x1 -> x0, blocking collectives: 37.4 us -> none  [per_device(): lax.psum((panel_sums, panel_counts), ('tm', 'panel'))]
    all_gather x2 -> x0, blocking collectives: 17.9 us -> none  [prefix_2(): everything = jax.tree.map(lambda part: lax.all_gather(part, axis), array)]
    psum x2 -> x0, waiting for transfers between devices: 8.1 us -> none  [the longest x1 8.08 us: per_device(): state_moment = lax.psum(local_moment, 'tm')]
  transfers between devices with their start and end apart: 8 -> 0, of which waited for: 5 -> 0; matrix products, arithmetic and copies ran while one was open for 36% -> 0% of each run, Pallas kernels for 0% -> 0%
where the time goes in v1:
time: 187 us
  Pallas kernels  165 us (88%)
  matrix products  9.27 us (5%)
  other arithmetic  6.84 us (4%)
  local copies, waits for them, and re-layouts  5.12 us (3%)
    pallas_call x1, Pallas kernels, smooth(): pl.pallas_call(functools.partial(smooth_kernel, segments, panels), out_sh...  93 us
    pallas_call x1, Pallas kernels, scatter_panel(): pl.pallas_call(functools.partial(scatter_kernel, panels), out_shape=jax.S...  33.6 us
    pallas_call x1, Pallas kernels, finish(): pl.pallas_call(functools.partial(finish_kernel, segments, panels), out_sh...  27.8 us
    pallas_call x1, Pallas kernels, local_tables(): pl.pallas_call(local_kernel, out_shape=(jax.ShapeDtypeStruct((width + PAD...  10.3 us

profile of v1, /device:TPU:0, one launch (start us, length us, event | category | flops | bytes accessed | tf_op | source)
XLA Modules:
  0.0 186.8 jit_solution(1504208974272624106)
XLA Ops:
  0.6 0.8 convert_bitcast_fusion
  1.4 0.7 broadcast_divide_fusion
  2.1 1.5 fusion.2
  3.7 1.1 fusion.18
  4.8 0.2 convert_multiply_fusion
  5.0 0.3 copy.15
  5.3 2.2 %fusion.10 = f32[4,256,256]{2,1,0:T(8,128)S(1)} fusion(f32[1024,4]{0,1:T(4,128)S(1)} %get-tuple-element.16, f32[1024,256]{0,1:T(8,128)S(1)} %copy.15, bf16[1024,256]{1,0:T(8,128)(2,1)S(1)} %copy-done.2), kind=kOutput, calls=%fused_computation.11 | convolution fusion | flops 3222274048 | bytes 2637824 | tf_op jit(solution)/shard_map/bi,is,ir->bsr/dot_general | solution.py:418
  7.5 1.3 pad_maximum_fusion.parts
  8.7 33.6 %scatter_panel.1.reduced = f32[384,256]{1,0:T(8,128)} custom-call(f32[4,384,256]{2,1,0:T(8,128)} %pad_maximum_fusion.parts), custom_call_target="tpu_custom_call" | custom-call | tf_op jit(solution)/shard_map/scatter_panel/pallas_call | solution.py:109
  42.4 0.8 copy.16.rho
  43.2 10.3 %local_tables.1 = (f32[264,256]{1,0:T(8,128)}, f32[7,256,256]{2,1,0:T(8,128)}, f32[128,256]{1,0:T(8,128)}) custom-call(f32[384,256]{1,0:T(8,128)} %scatter_panel.1.reduced, f32[256,1]{1,0:T(8,128)} %copy.16.rho), custom_call_target="tpu_custom_call" | custom-call | tf_op jit(solution)/shard_map/local_tables/pallas_call | solution.py:176
  53.5 93.0 %smooth.1 = f32[4,128,256]{2,1,0:T(8,128)} custom-call(f32[264,256]{1,0:T(8,128)} %get-tuple-element.9.pack, f32[7,256,256]{2,1,0:T(8,128)} %get-tuple-element.10.powers, f32[128,256]{1,0:T(8,128)} %get-tuple-element.11.partial, f32[1,256]{1,0:T(1,128)} %bitcast.45), custom_call_target="tpu_custom_call" | custom-call | tf_op jit(solution)/shard_map/smooth/pallas_call | solution.py:290
  146.6 2.4 %multiply_reduce_fusion = f32[1024]{0:T(1024)S(1)} fusion(f32[4,128,256]{2,1,0:T(8,128)} %smooth.1, f32[4,1024]{1,0:T(4,128)S(1)} %get-tuple-element.17, bf16[1024,256]{1,0:T(8,128)(2,1)S(1)} %copy-done.2, bf16[4,128,1024]{2,1,0:T(8,128)(2,1)S(1)} %bitcast.41), kind=kOutput, calls=%fused_computation.4 | convolution fusion | flops 1613757440 | bytes 2117632 | tf_op jit(solution)/shard_map/dot_general | solution.py:434
  149.3 0.7 maximum_maximum_fusion.sums
  150.0 0.7 convolution_multiply_fusion
  150.7 0.6 reshape.50.moment
  151.3 3.0 %fusion.13 = f32[256,1024]{1,0:T(8,128)} fusion(f32[4,128,256]{2,1,0:T(8,128)S(1)} %copy-done, f32[4,1024]{1,0:T(4,128)S(1)} %get-tuple-element.17, bf16[4,128,1024]{2,1,0:T(8,128)(2,1)S(1)} %bitcast.42), kind=kOutput, calls=%fused_computation.12 | convolution fusion | flops 1611923456 | bytes 2637824 | tf_op jit(solution)/shard_map/dot_general | solution.py:429
  154.3 27.8 %finish.1 = (f32[32,1024]{1,0:T(8,128)}, f32[32,24,128]{2,1,0:T(8,128)}) custom-call(f32[8,32,1024]{2,1,0:T(8,128)} %bitcast.43, f32[8,16,128]{2,1,0:T(8,128)} %reshape.50.moment, f32[8,128]{1,0:T(8,128)} %maximum_maximum_fusion.sums), custom_call_target="tpu_custom_call" | custom-call | tf_op jit(solution)/shard_map/finish/pallas_call | solution.py:384
  182.1 1.0 slice.12
  183.1 0.8 reshape.52
  183.9 0.9 slice_reduce_fusion
  184.8 0.5 fusion.22
  185.4 0.8 copy.21
  186.2 0.7 copy.22
  (22 shorter events, 0.4 us)
Async XLA Ops:
  0.6 3.0 %copy-start.2 = (bf16[1024,256]{1,0:T(8,128)(2,1)S(1)}, bf16[1024,256]{1,0:T(8,128)(2,1)}, u32[]{:S(2)}) copy-start(bf16[1024,256]{1,0:T(8,128)(2,1)} %param.8) | copy-start | bytes 1572868
  7.5 34.9 %copy-start.6 = (f32[256]{0:T(256)S(1)}, f32[256]{0:T(256)}, u32[]{:S(2)}) copy-start(f32[256]{0:T(256)} %param.10) | copy-start | bytes 3076
  42.4 104.2 %copy-start.1 = (bf16[512,1024]{1,0:T(8,128)(2,1)S(1)}, bf16[512,1024]{1,0:T(8,128)(2,1)}, u32[]{:S(2)}) copy-start(bf16[512,1024]{1,0:T(8,128)(2,1)} %param.6) | copy-start | bytes 3145732
  42.4 11.1 %copy-start.5 = (f32[256]{0:T(256)}, f32[256]{0:T(256)S(1)}, u32[]{:S(2)}) copy-start(f32[256]{0:T(256)S(1)} %broadcast_subtract_fusion) | copy-start | bytes 3076
  146.6 2.4 %copy-start.4 = (s32[4,1024]{1,0:T(4,128)S(1)}, s32[4,1024]{1,0:T(4,128)}, u32[]{:S(2)}) copy-start(s32[4,1024]{1,0:T(4,128)} %param.7) | copy-start | bytes 49156
  146.6 2.6 %copy-start.7 = (s32[8]{0:T(128)S(1)}, s32[8]{0:T(128)}, u32[]{:S(2)}) copy-start(s32[8]{0:T(128)} %param.11) | copy-start | bytes 100
  146.6 3.4 %copy-start = (f32[4,128,256]{2,1,0:T(8,128)S(1)}, f32[4,128,256]{2,1,0:T(8,128)}, u32[]{:S(2)}) copy-start(f32[4,128,256]{2,1,0:T(8,128)} %smooth.1) | copy-start | bytes 1572868
  182.1 4.1 %copy-start.3 = (f32[32,1024]{1,0:T(8,128)S(1)}, f32[32,1024]{1,0:T(8,128)}, u32[]{:S(2)}) copy-start(f32[32,1024]{1,0:T(8,128)} %get-tuple-element.25) | copy-start | bytes 393220

commit v2 on v1

--- a/solution.py
+++ b/solution.py
@@ -134,9 +134,15 @@
     return jnp.where(row < rows - offset, pltpu.roll(moved, rows - offset, 0), 0.0)
 
 
-def local_kernel(reduced, rho, pack, powers, values_out, stack):
-    width = reduced.shape[1]
-    gram = reduced[:width]
+def unfold(top, corner):
+    half = top.shape[0]
+    return jnp.concatenate([top, jnp.concatenate([top[:, half:].T, corner], axis=1)], axis=0)
+
+
+def local_kernel(reduced, rho, rho_row, pack, powers, values_out, stack):
+    width = rho.shape[0]
+    half = width // 2
+    gram = unfold(reduced[:, :width], reduced[:, width : width + half])
     eye = (
         lax.broadcasted_iota(jnp.int32, (width, width), 0)
         == lax.broadcasted_iota(jnp.int32, (width, width), 1)
@@ -157,7 +163,7 @@
     lax.while_loop(lambda level: level > 1e-5, step, ratio * ratio)
     guess = alpha * stack[:width]
     inverse = guess + mm(guess, (eye - guess) - mm(gram, guess))
-    values = mm(reduced[width:], inverse)
+    values = mm(reduced[:, width + half :], inverse)
     power = rho[...] * inverse
     for level in range(LEVELS):
         powers[level] = power
@@ -165,27 +171,31 @@
         values = values + shift_rows(both[width:], 1 << level, True)
         power = both[:width]
     values_out[...] = values
-    pack[:width] = power
+    scaled = power * rho_row[...]
+    pack[:half, :width] = scaled[:half]
+    pack[:half, width:] = scaled[half:, half:]
     row = lax.broadcasted_iota(jnp.int32, (PAD, width), 0)
-    pack[width:] = jnp.where(row == 0, pltpu.roll(values[BLOCK - PAD :], 1, 0), 0.0)
+    pack[half:, :width] = jnp.where(row == 0, pltpu.roll(values[BLOCK - PAD :], 1, 0), 0.0)
+    pack[half:, width:] = jnp.zeros((PAD, half), jnp.float32)
 
 
 def local_tables(reduced, persist):
-    width = reduced.shape[1]
+    width = persist.shape[0]
+    half = width // 2
     f32 = jnp.float32
     return pl.pallas_call(
         local_kernel,
         out_shape=(
-            jax.ShapeDtypeStruct((width + PAD, width), f32),
+            jax.ShapeDtypeStruct((half + PAD, width + half), f32),
             jax.ShapeDtypeStruct((LEVELS, width, width), f32),
             jax.ShapeDtypeStruct((BLOCK, width), f32),
         ),
-        in_specs=vmem(2),
+        in_specs=vmem(3),
         out_specs=tuple(vmem(3)),
         scratch_shapes=[pltpu.VMEM((2 * width, width), f32)],
         compiler_params=params(),
         name="local_tables",
-    )(reduced, persist[:, None])
+    )(reduced, persist[:, None], persist[None, :])
 
 
 def spread(first, powers, ahead):
@@ -204,6 +214,22 @@
     return rows
 
 
+def swap(source, target, send, recv, partner):
+    return pltpu.make_async_remote_copy(
+        src_ref=source,
+        dst_ref=target,
+        send_sem=send,
+        recv_sem=recv,
+        device_id={"tm": partner},
+        device_id_type=MESH,
+    )
+
+
+def chip_copy(source, target, d, send, recv, chip, chips, core):
+    peer = 2 * lax.rem(chip + d, chips) + core
+    return swap(source, target, send.at[d - 1], recv.at[d - 1], peer)
+
+
 def smooth_kernel(
     segments,
     panels,
@@ -212,46 +238,97 @@
     partial,
     rho,
     out,
+    landed,
     near,
     far,
     seg_pack,
+    pair_in,
+    pair_pack,
     own_first,
     firsts,
     seg_first,
-    seg_firsts,
+    pair_first,
+    chip_first,
+    chip_firsts,
     mine,
     near_send,
     near_recv,
+    pair_send,
+    pair_recv,
     far_send,
     far_recv,
 ):
-    width = pack.shape[1]
+    width = rho.shape[1]
+    half = width // 2
     place = lax.axis_index("panel")
     segment = lax.axis_index("tm")
+    chips, chip, core = segments // 2, segment // 2, lax.rem(segment, 2)
+    partner = segment + 1 - 2 * core
     greet([("panel", panels, place), ("tm", segments, segment)])
 
-    def gather(axis, n, me, source, target, stage):
-        send, recv = (near_send, near_recv) if axis == "panel" else (far_send, far_recv)
-        args = (axis, n, me, lambda peer: source, lambda i, d: target.at[i])
-        send_all(*args, send.at[stage], recv.at[stage])
-        target[me] = source[...]
-        wait_all(*args, send.at[stage], recv.at[stage])
+    def gather(source, target, stage):
+        args = ("panel", panels, place, lambda peer: source, lambda i, d: target.at[i])
+        send_all(*args, near_send.at[stage], near_recv.at[stage])
+        target[place] = source[...]
+        wait_all(*args, near_send.at[stage], near_recv.at[stage])
 
     row = lax.broadcasted_iota(jnp.int32, (PAD, width), 0)
     decay = rho[...]
-    gather("panel", panels, place, pack, near, 0)
+    gather(pack, landed, 0)
+    for k in range(panels):
+        near[k, :width] = unfold(landed[k, :half, :width], landed[k, :half, width:]) / decay
+        near[k, width:] = landed[k, half:, :width]
     whole = near[0]
     keep = (lax.broadcasted_iota(jnp.int32, (width + PAD, width), 0) >= width).astype(jnp.float32)
     for k in range(1, panels):
         whole = mm(whole, near[k, :width]) + keep * near[k]
     seg_pack[...] = whole
-    gather("tm", segments, segment, seg_pack, far, 0)
+    pair = swap(seg_pack, pair_in, pair_send.at[0], pair_recv.at[0], partner)
+    pair.start()
+    pair.wait()
+    first = jnp.where(core == 0, whole, pair_in[...])
+    second = jnp.where(core == 0, pair_in[...], whole)
+    joined = mm(first, second[:width]) + keep * second
+    pair_pack[: width + PAD] = joined
+    pair_pack[width + PAD :] = jnp.zeros((PAD, width), jnp.float32)
+    share = (width + 2 * PAD) // 2
+    rows = pl.ds(pl.multiple_of(core * share, 8), share)
+
+    def out_copy(d, slot):
+        return chip_copy(
+            pair_pack.at[rows],
+            far.at[slot, rows],
+            d,
+            far_send.at[0],
+            far_recv.at[0],
+            chip,
+            chips,
+            core,
+        )
+
+    other = pl.ds(pl.multiple_of((1 - core) * share, 8), share)
+
+    def relay(d, part):
+        slot = far.at[lax.rem(chip + chips - d, chips), part]
+        return swap(slot, slot, far_send.at[1, d - 1], far_recv.at[1, d - 1], partner)
+
+    for d in range(1, chips):
+        out_copy(d, chip).start()
+    far[chip] = pair_pack[...]
+    for d in range(1, chips):
+        out_copy(d, lax.rem(chip + chips - d, chips)).wait_recv()
+        relay(d, rows).start()
+    for d in range(1, chips):
+        relay(d, other).wait_recv()
+        relay(d, rows).wait_send()
+        out_copy(d, chip).wait_send()
 
     def far_ahead(k, state):
-        new = mm(state, far[k, :width]) + far[k, width:]
-        return jnp.where(k < segment, new, state)
-
-    state = lax.fori_loop(0, segments - 1, far_ahead, jnp.zeros((PAD, width), jnp.float32))
+        new = mm(state, far[k, :width]) + far[k, width : width + PAD]
+        return jnp.where(k < chip, new, state)
+
+    state = lax.fori_loop(0, chips - 1, far_ahead, jnp.zeros((PAD, width), jnp.float32))
+    state = jnp.where(core == 1, mm(state, pair_in[:width]) + pair_in[width:], state)
     for k in range(panels - 1):
         state = jnp.where(k < place, mm(state, near[k, :width]) + near[k, width:], state)
 
@@ -263,63 +340,101 @@
     for level in range(LEVELS):
         values = values + shift_rows(mm(values, powers[level]), 1 << level, False)
     own_first[...] = jnp.where(row == 0, values[:PAD], 0.0)
-    gather("panel", panels, place, own_first, firsts, 1)
+    gather(own_first, firsts, 1)
     total = firsts[panels - 1]
     for k in range(panels - 2, -1, -1):
         total = mm(total, near[k, :width]) + firsts[k]
-    seg_first[...] = total * decay
-    gather("tm", segments, segment, seg_first, seg_firsts, 1)
+    total = total * decay
+    seg_first[...] = total
+    pair = swap(seg_first, pair_first, pair_send.at[1], pair_recv.at[1], partner)
+    pair.start()
+    pair.wait()
+    early = jnp.where(core == 0, total, pair_first[...])
+    late = jnp.where(core == 0, pair_first[...], total)
+    early_map = jnp.where(core == 0, seg_pack[:width], pair_in[:width])
+    both = mm_t(late, early_map) + early
+    chip_first[...] = both
+
+    def first_copy(d, slot):
+        return chip_copy(
+            chip_first,
+            chip_firsts.at[slot],
+            d,
+            far_send.at[2],
+            far_recv.at[2],
+            chip,
+            chips,
+            core,
+        )
+
+    for d in range(1, chips):
+        first_copy(d, chip).start()
+    chip_firsts[chip] = both
+    for d in range(1, chips):
+        first_copy(d, lax.rem(chip + chips - d, chips)).wait_recv()
+        first_copy(d, chip).wait_send()
 
     def far_back(j, state):
-        k = segments - 1 - j
-        new = mm_t(state, far[k, :width]) + seg_firsts[k]
-        return jnp.where(k > segment, new, state)
-
-    state = lax.fori_loop(0, segments - 1, far_back, jnp.zeros((PAD, width), jnp.float32))
+        k = chips - 1 - j
+        new = mm_t(state, far[k, :width]) + chip_firsts[k]
+        return jnp.where(k > chip, new, state)
+
+    state = lax.fori_loop(0, chips - 1, far_back, jnp.zeros((PAD, width), jnp.float32))
+    state = jnp.where(core == 0, mm_t(state, pair_in[:width]) + pair_first[...], state)
     state = state / decay
     for k in range(panels - 1, 0, -1):
         state = jnp.where(k > place, mm(state, near[k, :width]) + firsts[k], state)
     mine[...] = values + spread(state, powers, False)
-    gather("panel", panels, place, mine, out, 2)
+    gather(mine, out, 2)
 
 
 def smooth(pack, powers, partial, persist):
-    width = pack.shape[1]
+    width = persist.shape[0]
     segments, panels = lax.axis_size("tm"), lax.axis_size("panel")
+    chips = segments // 2
     f32 = jnp.float32
+    dma = pltpu.SemaphoreType.DMA
     return pl.pallas_call(
         functools.partial(smooth_kernel, segments, panels),
         out_shape=jax.ShapeDtypeStruct((panels, BLOCK, width), f32),
         in_specs=vmem(4),
         out_specs=pl.BlockSpec(memory_space=pltpu.VMEM),
         scratch_shapes=[
+            pltpu.VMEM((panels,) + pack.shape, f32),
             pltpu.VMEM((panels, width + PAD, width), f32),
-            pltpu.VMEM((segments, width + PAD, width), f32),
+            pltpu.VMEM((chips, width + 2 * PAD, width), f32),
             pltpu.VMEM((width + PAD, width), f32),
+            pltpu.VMEM((width + PAD, width), f32),
+            pltpu.VMEM((width + 2 * PAD, width), f32),
             pltpu.VMEM((PAD, width), f32),
             pltpu.VMEM((panels, PAD, width), f32),
             pltpu.VMEM((PAD, width), f32),
-            pltpu.VMEM((segments, PAD, width), f32),
+            pltpu.VMEM((PAD, width), f32),
+            pltpu.VMEM((PAD, width), f32),
+            pltpu.VMEM((chips, PAD, width), f32),
             pltpu.VMEM((BLOCK, width), f32),
-            pltpu.SemaphoreType.DMA((3, panels - 1)),
-            pltpu.SemaphoreType.DMA((3, panels - 1)),
-            pltpu.SemaphoreType.DMA((2, segments - 1)),
-            pltpu.SemaphoreType.DMA((2, segments - 1)),
+            dma((3, panels - 1)),
+            dma((3, panels - 1)),
+            dma((2,)),
+            dma((2,)),
+            dma((3, chips - 1)),
+            dma((3, chips - 1)),
         ],
         compiler_params=params(2),
         name="smooth",
     )(pack, powers, partial, persist[None, :])
 
 
-def finish_kernel(
-    segments, panels, cross, moment, sums, out, gathered, landed, moments, bundle, *sems
-):
-    c_send, c_recv, m_send, m_recv, g_send, g_recv = sems
+def finish_kernel(segments, panels, parts, sums, out, moments, variances, *scratch):
+    pair_in, merged, landed, moment, tallies = scratch[:5]
+    p_send, p_recv, c_send, c_recv, m_send, m_recv, g_send, g_recv = scratch[5:]
     place = lax.axis_index("panel")
     segment = lax.axis_index("tm")
+    chips, chip, core = segments // 2, segment // 2, lax.rem(segment, 2)
+    partner = segment + 1 - 2 * core
     devices = segments * panels
     me = place * segments + segment
-    rows = moment.shape[1]
+    series = out.shape[1]
     barrier = pltpu.get_barrier_semaphore()
 
     def where(d):
@@ -333,22 +448,13 @@
     lax.fori_loop(1, devices, hello, 0)
     pl.semaphore_wait(barrier, devices - 1)
 
-    m_args = ("tm", segments, segment, lambda i: moment.at[i], lambda i, d: moments.at[d - 1])
-    c_args = ("tm", segments, segment, lambda i: cross.at[i], lambda i, d: landed.at[d - 1])
-    send_all(*m_args, m_send, m_recv)
-    send_all(*c_args, c_send, c_recv)
-    own = moment[segment]
-    wait_all(*m_args, m_send, m_recv)
-    for d in range(segments - 1):
-        own = own + moments[d]
-    bundle[:rows] = own
-    bundle[rows:] = sums[...]
-    gathered[me] = bundle[...]
-
-    def copy(d, slot):
+    pair = swap(parts.at[:, 1 - core], pair_in, p_send.at[0], p_recv.at[0], partner)
+    pair.start()
+
+    def tally(d, slot):
         return pltpu.make_async_remote_copy(
-            src_ref=bundle,
-            dst_ref=gathered.at[slot],
+            src_ref=sums,
+            dst_ref=tallies.at[slot],
             send_sem=g_send.at[d - 1],
             recv_sem=g_recv.at[d - 1],
             device_id=where(d),
@@ -356,45 +462,71 @@
         )
 
     def push(d, unused):
-        copy(d, me).start()
+        tally(d, me).start()
         return unused
 
     lax.fori_loop(1, devices, push, 0)
-    total = cross[segment]
-    wait_all(*c_args, c_send, c_recv)
-    for d in range(segments - 1):
-        total = total + landed[d]
-    out[...] = total
+    tallies[me] = sums[...]
+    pair.wait()
+    merged[...] = parts[:, core] + pair_in[...]
+
+    def part_copy(d):
+        to = lax.rem(chip + d, chips)
+        return chip_copy(
+            merged.at[to], landed.at[d - 1], d, c_send, c_recv, chip, chips, core
+        )
+
+    for d in range(1, chips):
+        part_copy(d).start()
+    total = merged[chip]
+    for d in range(1, chips):
+        part_copy(d).wait()
+        total = total + landed[d - 1]
+    out[...] = total[:, :series]
+    moment[...] = total[:, series:]
+    args = ("tm", segments, segment, lambda i: moment, lambda i, d: moments.at[i])
+    send_all(*args, m_send, m_recv)
+    moments[segment] = moment[...]
 
     def pull(d, unused):
-        got = copy(d, lax.rem(me + devices - d, devices))
+        got = tally(d, lax.rem(me + devices - d, devices))
         got.wait_recv()
         got.wait_send()
         return unused
 
     lax.fori_loop(1, devices, pull, 0)
-
-
-def finish(cross, moment, sums):
+    totals = jnp.sum(tallies[...], axis=0)
+    variances[...] = totals[0:1] / jnp.maximum(totals[1:2], 1.0)
+    wait_all(*args, m_send, m_recv)
+
+
+def finish(parts, sums, series):
     segments, panels = lax.axis_size("tm"), lax.axis_size("panel")
     devices = segments * panels
+    chips = segments // 2
+    rows, columns = parts.shape[2:]
+    width = columns - series
     f32 = jnp.float32
-    rows = moment.shape[1] + sums.shape[0]
     dma = pltpu.SemaphoreType.DMA
     return pl.pallas_call(
         functools.partial(finish_kernel, segments, panels),
         out_shape=(
-            jax.ShapeDtypeStruct(cross.shape[1:], f32),
-            jax.ShapeDtypeStruct((devices, rows, 128), f32),
+            jax.ShapeDtypeStruct((rows, series), f32),
+            jax.ShapeDtypeStruct((segments, rows, width), f32),
+            jax.ShapeDtypeStruct((1, 128), f32),
         ),
-        in_specs=vmem(3),
-        out_specs=tuple(vmem(2)),
+        in_specs=vmem(2),
+        out_specs=tuple(vmem(3)),
         scratch_shapes=[
-            pltpu.VMEM((segments - 1,) + cross.shape[1:], f32),
-            pltpu.VMEM((segments - 1,) + moment.shape[1:], f32),
-            pltpu.VMEM((rows, 128), f32),
-            dma((segments - 1,)),
-            dma((segments - 1,)),
+            pltpu.VMEM((chips, rows, columns), f32),
+            pltpu.VMEM((chips, rows, columns), f32),
+            pltpu.VMEM((chips - 1, rows, columns), f32),
+            pltpu.VMEM((rows, width), f32),
+            pltpu.VMEM((devices,) + sums.shape, f32),
+            dma((1,)),
+            dma((1,)),
+            dma((chips - 1,)),
+            dma((chips - 1,)),
             dma((segments - 1,)),
             dma((segments - 1,)),
             dma((devices - 1,)),
@@ -402,7 +534,7 @@
         ],
         compiler_params=params(3),
         name="finish",
-    )(cross, moment, sums)
+    )(parts, sums)
 
 
 def per_device(observed, present, loadings, noise_var, decay_rate, panel_of_block):
@@ -419,7 +551,15 @@
     obs_kept = observed.astype(jnp.float32).reshape(nblocks, BLOCK, series) * kept_mask[:, None, :]
     projected = jnp.dot((obs_kept * inv_noise).reshape(time_rows, series), loads, precision=HIGH)
     persist = 1.0 - decay_rate
-    parts = jnp.concatenate([gram_sum, projected.reshape(nblocks, BLOCK, width)], axis=1)
+    half = width // 2
+    parts = jnp.concatenate(
+        [
+            gram_sum[:, :half],
+            gram_sum[:, half:, half:],
+            projected.reshape(nblocks, BLOCK, width),
+        ],
+        axis=2,
+    )
     reduced = scatter_panel(parts)
     pack, powers, partial = local_tables(reduced, persist)
     smoothed = smooth(pack, powers, partial, persist).reshape(time_rows, width)
@@ -427,9 +567,7 @@
     total_time = time_rows * segments
     flat_kept = obs_kept.reshape(time_rows, series)
     cross = jnp.dot(smoothed.T, flat_kept, precision=HIGH) / math.sqrt(total_time)
-    part = width // panels
-    columns = lax.dynamic_slice_in_dim(smoothed, lax.axis_index("panel") * part, part, axis=1)
-    moment = jnp.dot(columns.T, smoothed, precision=HIGH) / total_time
+    moment = jnp.dot(smoothed.T, smoothed, precision=HIGH) / total_time
     fitted = (
         jnp.dot(smoothed, loads.T, precision=HIGH).reshape(nblocks, BLOCK, series)
         * kept_mask[:, None, :]
@@ -447,15 +585,11 @@
         ]
     )
     sums = jnp.concatenate([sums, jnp.zeros((PAD - 2, 128), jnp.float32)], axis=0)
-    moment_rows = part * width // segments // 128
-    loading_moment, gathered = finish(
-        cross.reshape(segments, width // segments, series),
-        moment.reshape(segments, moment_rows, 128),
-        sums,
-    )
-    state_moment = gathered[:, :moment_rows].reshape(width, width)
-    totals = jnp.sum(gathered[:, moment_rows : moment_rows + 2, :PANELS], axis=0)
-    panel_var = totals[0] / jnp.maximum(totals[1], 1.0)
+    both = jnp.concatenate([cross, moment], axis=1)
+    both = both.reshape(segments // 2, 2, width // segments, series + width)
+    loading_moment, moments, variances = finish(both, sums, series)
+    state_moment = moments.reshape(width, width)
+    panel_var = variances[0, :PANELS]
     return (smoothed, loading_moment, state_moment, panel_var)
 
 

time: 187 us -> 163 us (0.87)
  Pallas kernels: 165 us -> 138 us
    pallas_call x1, Pallas kernels: 93 us -> 73.5 us  [smooth(): pl.pallas_call(functools.partial(smooth_kernel, segments, panels), out_sh...]
    pallas_call x1, Pallas kernels: 33.6 us -> 29.4 us  [scatter_panel(): pl.pallas_call(functools.partial(scatter_kernel, panels), out_shape=jax.S...]
    pallas_call x1, Pallas kernels: 27.8 us -> 25.1 us  [finish(): pl.pallas_call(functools.partial(finish_kernel, segments, panels), out_sh...]
    unnamed x18 -> x17, local copies, waits for them, and re-layouts: 1.49 us -> 4.06 us
    dot_general x1, matrix products: 2.16 us -> 4.08 us  [per_device(): jnp.einsum('bi,is,ir->bsr', kept_mask, weighted, loads, precision=HIGH)]
where the time goes in v2:
time: 163 us; the launch traced here: 162 us
  Pallas kernels  138 us (85%)
  matrix products  10.5 us (6%)
  other arithmetic  6.42 us (4%)
  local copies, waits for them, and re-layouts  6.14 us (4%)
    pallas_call x1, Pallas kernels, smooth(): pl.pallas_call(functools.partial(smooth_kernel, segments, panels), out_sh...  73.5 us
    pallas_call x1, Pallas kernels, scatter_panel(): pl.pallas_call(functools.partial(scatter_kernel, panels), out_shape=jax.S...  29.4 us
    pallas_call x1, Pallas kernels, finish(): pl.pallas_call(functools.partial(finish_kernel, segments, panels), out_sh...  25.1 us
    pallas_call x1, Pallas kernels, local_tables(): pl.pallas_call(local_kernel, out_shape=(jax.ShapeDtypeStruct((half + PAD,...  10.4 us
    dot_general x1, matrix products, per_device(): jnp.einsum('bi,is,ir->bsr', kept_mask, weighted, loads, precision=HIGH)  4.08 us
    unnamed x17, local copies, waits for them, and re-layouts  4.06 us

profile of v2, /device:TPU:0, one launch (start us, length us, event | category | flops | bytes accessed | tf_op | source)
XLA Modules:
  0.0 162.4 jit_solution(156789479863554323)
XLA Ops:
  0.6 0.8 convert_bitcast_fusion
  1.4 0.7 broadcast_divide_fusion
  2.1 1.5 fusion.2
  3.7 1.1 fusion.19
  4.8 0.2 convert_multiply_fusion
  5.0 4.1 %fusion.10 = f32[4,256,256]{2,1,0:T(8,128)S(1)} fusion(f32[1024,4]{0,1:T(4,128)S(1)} %get-tuple-element.18, f32[1024,256]{1,0:T(8,128)S(1)} %convert_multiply_fusion, bf16[1024,256]{1,0:T(8,128)(2,1)S(1)} %copy-done.2), kind=kOutput, calls=%fused_computation.10 | convolution fusion | flops 3222274048 | bytes 2637824 | tf_op jit(solution)/shard_map/bi,is,ir->bsr/dot_general | solution.py:550
  9.1 1.2 pad_maximum_fusion.parts
  10.3 29.4 %scatter_panel.1.reduced = f32[128,640]{1,0:T(8,128)} custom-call(f32[4,128,640]{2,1,0:T(8,128)} %pad_maximum_fusion.parts), custom_call_target="tpu_custom_call" | custom-call | tf_op jit(solution)/shard_map/scatter_panel/pallas_call | solution.py:109
  39.7 0.8 copy.23.rho
  40.5 10.4 %local_tables.1 = (f32[136,384]{1,0:T(8,128)}, f32[7,256,256]{2,1,0:T(8,128)}, f32[128,256]{1,0:T(8,128)}) custom-call(f32[128,640]{1,0:T(8,128)} %scatter_panel.1.reduced, f32[256,1]{1,0:T(8,128)} %copy.23.rho, f32[1,256]{1,0:T(1,128)} %bitcast.52), custom_call_target="tpu_custom_call" | custom-call | tf_op jit(solution)/shard_map/local_tables/pallas_call | solution.py:186
  50.9 73.5 %smooth.1 = f32[4,128,256]{2,1,0:T(8,128)} custom-call(f32[136,384]{1,0:T(8,128)} %get-tuple-element.10.pack, f32[7,256,256]{2,1,0:T(8,128)} %get-tuple-element.11.powers, f32[128,256]{1,0:T(8,128)} %get-tuple-element.12.partial, f32[1,256]{1,0:T(1,128)} %bitcast.53), custom_call_target="tpu_custom_call" | custom-call | tf_op jit(solution)/shard_map/smooth/pallas_call | solution.py:397
  124.5 2.4 %multiply_reduce_fusion = f32[1024]{0:T(1024)S(1)} fusion(f32[4,128,256]{2,1,0:T(8,128)} %smooth.1, f32[4,1024]{1,0:T(4,128)S(1)} %get-tuple-element.19, bf16[1024,256]{1,0:T(8,128)(2,1)S(1)} %copy-done.2, bf16[4,128,1024]{2,1,0:T(8,128)(2,1)S(1)} %bitcast.48), kind=kOutput, calls=%fused_computation.4 | convolution fusion | flops 1613757440 | bytes 2117632 | tf_op jit(solution)/shard_map/dot_general | solution.py:572
  126.9 0.1 bitcast_reduce_fusion
  127.1 0.1 select_reduce_fusion.1
  127.2 0.1 pad.2.clone
  127.2 0.7 maximum_maximum_fusion.sums
  127.9 2.0 %fusion.13 = f32[256,1024]{1,0:T(8,128)S(1)} fusion(f32[4,128,256]{2,1,0:T(8,128)S(1)} %copy-done, f32[4,1024]{1,0:T(4,128)S(1)} %get-tuple-element.19, bf16[4,128,1024]{2,1,0:T(8,128)(2,1)S(1)} %bitcast.49), kind=kOutput, calls=%fused_computation.13 | convolution fusion | flops 1611923456 | bytes 2637824 | tf_op jit(solution)/shard_map/dot_general | solution.py:569
  129.9 1.0 fusion.16
  130.9 1.2 pad_maximum_fusion.1
  132.1 25.1 %finish.1 = (f32[32,1024]{1,0:T(8,128)}, f32[8,32,256]{2,1,0:T(8,128)}, f32[1,128]{1,0:T(1,128)}) custom-call(f32[4,2,32,1280]{3,2,1,0:T(8,128)} %bitcast.47, f32[8,128]{1,0:T(8,128)} %maximum_maximum_fusion.sums), custom_call_target="tpu_custom_call" | custom-call | tf_op jit(solution)/shard_map/finish/pallas_call | solution.py:511
  157.2 1.1 slice_bitcast_fusion
  158.3 0.8 copy.37
  159.1 1.6 copy.38
  160.7 1.7 %copy.39 = f32[256,256]{1,0:T(8,128)} copy(f32[256,256]{1,0:T(8,128)} %bitcast.50) | data formatting | bytes 524288
  (19 shorter events, 0.1 us)
Async XLA Ops:
  0.6 3.0 %copy-start.2 = (bf16[1024,256]{1,0:T(8,128)(2,1)S(1)}, bf16[1024,256]{1,0:T(8,128)(2,1)}, u32[]{:S(2)}) copy-start(bf16[1024,256]{1,0:T(8,128)(2,1)} %param.8) | copy-start | bytes 1572868
  9.1 30.5 %copy-start.5 = (f32[256]{0:T(256)S(1)}, f32[256]{0:T(256)}, u32[]{:S(2)}) copy-start(f32[256]{0:T(256)} %param.10) | copy-start | bytes 3076
  10.3 114.2 %copy-start.1 = (bf16[512,1024]{1,0:T(8,128)(2,1)S(1)}, bf16[512,1024]{1,0:T(8,128)(2,1)}, u32[]{:S(2)}) copy-start(bf16[512,1024]{1,0:T(8,128)(2,1)} %param.6) | copy-start | bytes 3145732
  39.7 0.8 copy-start.4
  124.4 2.4 %copy-start.3 = (s32[4,1024]{1,0:T(4,128)S(1)}, s32[4,1024]{1,0:T(4,128)}, u32[]{:S(2)}) copy-start(s32[4,1024]{1,0:T(4,128)} %param.7) | copy-start | bytes 49156
  124.5 2.6 %copy-start.6 = (s32[8]{0:T(128)S(1)}, s32[8]{0:T(128)}, u32[]{:S(2)}) copy-start(s32[8]{0:T(128)} %param.11) | copy-start | bytes 100
  124.5 3.4 %copy-start = (f32[4,128,256]{2,1,0:T(8,128)S(1)}, f32[4,128,256]{2,1,0:T(8,128)}, u32[]{:S(2)}) copy-start(f32[4,128,256]{2,1,0:T(8,128)} %smooth.1) | copy-start | bytes 1572868
